TPU v7x, 32 devices: a whole 2x2x4 slice. The times are simulated.
32 devices in a mesh: rep: 4 (over x, core), row: 2 (over y), col: 4 (over z).
Axes of the slice: x: 2, y: 2, z: 4, core: 2. Of those that a mesh axis runs over, the one named last changes fastest.
Arguments:
- spin_init: bfloat16 [256, 8192], P('rep', 'row'), may hold values from -1 to 1, as said below
- couplings: bfloat16 [2, 4, 1024, 8192], P(None, 'col', None, 'row'), may hold values from -1 to 1, as said below
- flip_noise: float32 [10, 256, 8192], P(None, 'rep', 'row'), may hold values from 0 to 17, as said below
- colors: int32 [8192], P('row'), may hold values 0 or 1
- beta_steps: int32 [256], replicated, may hold values from 96 to 1024
- partners: int32 [256], replicated, may hold values from 0 to 255, as said below
- swap_noise: float32 [256], replicated, may hold values from 0 to 17, as said below
Outputs:
- spins_out: bfloat16 [256, 8192], P('rep', 'row')
- energies: float32 [256], P('rep')
Inputs may be any that keep to these rules, and one draw needn't show every extreme that they name: `spin_init`: every entry is -1 or +1. `couplings`: the 8192 x 8192 matrix is symmetric, zero on its diagonal, and every other entry is -1 or +1. `flip_noise`: independent exponential variates of mean one. `swap_noise`: independent exponential variates of mean one. Pairs slots: partners[partners[r]] = r and partners[r] != r for every slot.
All inputs are finite; a program needn't handle non-finite values. No bound on the sum of `colors` on one device may be relied on, other than what follows from the above.
Results may differ from a plain program's by a relative error of at most 0.001.
Values may be sent and summed in bfloat16 or wider, within the bound.
A program may use at most 64 MiB of HBM per device.

v0:
```python
import math
import jax
import jax.numpy as jnp
from jax import lax
from jax.sharding import PartitionSpec as P

N = 8192
SWEEPS = 10


def metropolis(spin_state, fields, parity, color_part, noise_part, beta_col):
    values = spin_state.astype(jnp.float32)
    energy_cost = beta_col * (values * fields) * (1.0 / 16384.0)
    flipped = (color_part == parity)[None, :] & (energy_cost < noise_part)
    return jnp.where(flipped, -values, values).astype(jnp.bfloat16)


def partial_fields(strided, coupling_block):
    return jnp.dot(strided, coupling_block, preferred_element_type=jnp.float32)


def per_device(spin_init, couplings, flip_noise, colors, beta_steps, partners, swap_noise):
    rep_dev, row_width = spin_init.shape
    col_count = lax.axis_size("col")
    col_index = lax.axis_index("col")
    rep_index = lax.axis_index("rep")
    piece_size = row_width // col_count
    coupling_block = couplings.reshape(-1, row_width)
    beta_col = lax.dynamic_slice_in_dim(beta_steps, rep_index * rep_dev, rep_dev).astype(
        jnp.float32
    )[:, None]
    color_part = lax.dynamic_slice_in_dim(colors, col_index * piece_size, piece_size)
    noise_part = lax.dynamic_slice_in_dim(flip_noise, col_index * piece_size, piece_size, 2)

    def strided_of(spin_state):
        return lax.all_gather(spin_state, "row", axis=1, tiled=True)

    def one_sweep(step_index, spin_state):
        terms = partial_fields(strided_of(spin_state), coupling_block)
        fields = lax.psum_scatter(terms, "col", scatter_dimension=1, tiled=True)
        return metropolis(
            spin_state, fields, step_index % 2, color_part, noise_part[step_index], beta_col
        )

    start_pieces = lax.dynamic_slice_in_dim(spin_init, col_index * piece_size, piece_size, 1)
    final_pieces = lax.fori_loop(0, SWEEPS, one_sweep, start_pieces)
    strided = strided_of(final_pieces)
    final_rows = lax.all_gather(final_pieces, "col", axis=1, tiled=True)
    every_spins = lax.all_gather(final_rows, "rep", axis=0, tiled=True)
    final_partial = partial_fields(strided, coupling_block)
    row_values = final_rows.astype(jnp.float32)
    final_local = lax.psum(final_partial, "col")
    total_sum = lax.psum(jnp.sum(row_values * final_local, axis=1), "row")
    energy = -0.5 * total_sum
    every_energy = lax.all_gather(energy, "rep", axis=0, tiled=True)
    slot_ids = rep_index * rep_dev + jnp.arange(rep_dev, dtype=jnp.int32)
    mate_ids = lax.dynamic_slice_in_dim(partners, rep_index * rep_dev, rep_dev)
    all_betas = beta_steps.astype(jnp.float32)
    mate_energy = every_energy[mate_ids]
    swap_gain = (
        (beta_col[:, 0] - all_betas[mate_ids])
        * (energy - mate_energy)
        * (1.0 / (64.0 * N * math.sqrt(N)))
    )
    accept = swap_gain + swap_noise[jnp.minimum(slot_ids, mate_ids)] > 0.0
    spins_out = jnp.where(accept[:, None], every_spins[mate_ids], final_rows)
    energies = jnp.where(accept, mate_energy, energy) * (1.0 / (N * math.sqrt(N)))
    return (spins_out, energies)


def solution(mesh):
    in_specs = (
        P("rep", "row"),
        P(None, "col", None, "row"),
        P(None, "rep", "row"),
        P("row"),
        P(),
        P(),
        P(),
    )
    out_specs = (P("rep", "row"), P("rep"))
    return jax.shard_map(
        per_device, mesh=mesh, in_specs=in_specs, out_specs=out_specs, check_vma=False
    )
```

profile of v0, /device:TPU:0, one launch (start us, length us, event | category | flops | bytes accessed | tf_op | source)
XLA Modules:
  0.0 540.9 jit_solution(17251068194962414624)
XLA Ops:
  12.4 431.6 %while.15 = (s32[]{:T(128)}, bf16[64,1024]{1,0:T(8,128)(2,1)S(1)}, s32[1024]{0:T(1024)S(1)}, f32[64,1]{0,1:T(1,128)S(1)}, bf16[2048,4096]{1,0:T(8,128)(2,1)}, /*...) while((s32[]{:T(128)}, bf16[64,1024]{1,0:T(8,128)(2,1)S(1)}, s32[1024]{0:T(1024)S(1)}, ...), condition=%wide.region_2.3_spmd, body=%wide.region_0.2_spmd.sunk | while | flops 1074332672 | bytes 23206348 | solution.py:46
  12.4 7.1 %all_gather.27 = bf16[64,2048]{1,0:T(8,128)(2,1)S(1)} all-gather(bf16[64,1024]{1,0:T(8,128)(2,1)S(1)} %get-tuple-element.221), channel_id=1, replica_groups=mesh['rep'=4,'row'=2,'col'=4] {'row'}, dimensions={1}, use_global_device_ids=true | all-gather | bytes 393216 | tf_op jit(solution)/shard_map/while/body/eval_jaxpr/all_gather | solution.py:36
  19.6 9.8 %fusion.17 = f32[64,4096]{1,0:T(8,128)} fusion(bf16[64,2048]{1,0:T(8,128)(2,1)S(1)} %all_gather.27, bf16[2048,4096]{1,0:T(8,128)(2,1)} %get-tuple-element.233), kind=kOutput, calls=%fused_computation.24.clone.1 | convolution fusion | flops 1073741824 | bytes 18087936 | tf_op jit(solution)/shard_map/while/body/eval_jaxpr/dot_general | solution.py:19
  29.4 28.9 %reduce-scatter.2.cloned.1.call-done = f32[64,1024]{1,0:T(8,128)} async-done(((f32[64,4096]{1,0:T(8,128)}), f32[64,1024]{1,0:T(8,128)}) %reduce-scatter.2.cloned.1.call-update) | async-done | bytes 262160 | tf_op jit(solution)/shard_map/while/body/eval_jaxpr/reduce_scatter | solution.py:40
  59.4 5.6 %all_gather.27 = bf16[64,2048]{1,0:T(8,128)(2,1)S(1)} all-gather(bf16[64,1024]{1,0:T(8,128)(2,1)S(1)} %get-tuple-element.221), channel_id=1, replica_groups=mesh['rep'=4,'row'=2,'col'=4] {'row'}, dimensions={1}, use_global_device_ids=true | all-gather | bytes 393216 | tf_op jit(solution)/shard_map/while/body/eval_jaxpr/all_gather | solution.py:36
  65.1 9.8 %fusion.17 = f32[64,4096]{1,0:T(8,128)} fusion(bf16[64,2048]{1,0:T(8,128)(2,1)S(1)} %all_gather.27, bf16[2048,4096]{1,0:T(8,128)(2,1)} %get-tuple-element.233), kind=kOutput, calls=%fused_computation.24.clone.1 | convolution fusion | flops 1073741824 | bytes 18087936 | tf_op jit(solution)/shard_map/while/body/eval_jaxpr/dot_general | solution.py:19
  74.9 26.1 %reduce-scatter.2.cloned.1.call-done = f32[64,1024]{1,0:T(8,128)} async-done(((f32[64,4096]{1,0:T(8,128)}), f32[64,1024]{1,0:T(8,128)}) %reduce-scatter.2.cloned.1.call-update) | async-done | bytes 262160 | tf_op jit(solution)/shard_map/while/body/eval_jaxpr/reduce_scatter | solution.py:40
  102.2 5.6 %all_gather.27 = bf16[64,2048]{1,0:T(8,128)(2,1)S(1)} all-gather(bf16[64,1024]{1,0:T(8,128)(2,1)S(1)} %get-tuple-element.221), channel_id=1, replica_groups=mesh['rep'=4,'row'=2,'col'=4] {'row'}, dimensions={1}, use_global_device_ids=true | all-gather | bytes 393216 | tf_op jit(solution)/shard_map/while/body/eval_jaxpr/all_gather | solution.py:36
  107.8 9.8 %fusion.17 = f32[64,4096]{1,0:T(8,128)} fusion(bf16[64,2048]{1,0:T(8,128)(2,1)S(1)} %all_gather.27, bf16[2048,4096]{1,0:T(8,128)(2,1)} %get-tuple-element.233), kind=kOutput, calls=%fused_computation.24.clone.1 | convolution fusion | flops 1073741824 | bytes 18087936 | tf_op jit(solution)/shard_map/while/body/eval_jaxpr/dot_general | solution.py:19
  117.6 26.1 %reduce-scatter.2.cloned.1.call-done = f32[64,1024]{1,0:T(8,128)} async-done(((f32[64,4096]{1,0:T(8,128)}), f32[64,1024]{1,0:T(8,128)}) %reduce-scatter.2.cloned.1.call-update) | async-done | bytes 262160 | tf_op jit(solution)/shard_map/while/body/eval_jaxpr/reduce_scatter | solution.py:40
  144.9 5.6 %all_gather.27 = bf16[64,2048]{1,0:T(8,128)(2,1)S(1)} all-gather(bf16[64,1024]{1,0:T(8,128)(2,1)S(1)} %get-tuple-element.221), channel_id=1, replica_groups=mesh['rep'=4,'row'=2,'col'=4] {'row'}, dimensions={1}, use_global_device_ids=true | all-gather | bytes 393216 | tf_op jit(solution)/shard_map/while/body/eval_jaxpr/all_gather | solution.py:36
  150.5 9.8 %fusion.17 = f32[64,4096]{1,0:T(8,128)} fusion(bf16[64,2048]{1,0:T(8,128)(2,1)S(1)} %all_gather.27, bf16[2048,4096]{1,0:T(8,128)(2,1)} %get-tuple-element.233), kind=kOutput, calls=%fused_computation.24.clone.1 | convolution fusion | flops 1073741824 | bytes 18087936 | tf_op jit(solution)/shard_map/while/body/eval_jaxpr/dot_general | solution.py:19
  160.4 26.2 %reduce-scatter.2.cloned.1.call-done = f32[64,1024]{1,0:T(8,128)} async-done(((f32[64,4096]{1,0:T(8,128)}), f32[64,1024]{1,0:T(8,128)}) %reduce-scatter.2.cloned.1.call-update) | async-done | bytes 262160 | tf_op jit(solution)/shard_map/while/body/eval_jaxpr/reduce_scatter | solution.py:40
  193.3 9.8 %fusion.17 = f32[64,4096]{1,0:T(8,128)} fusion(bf16[64,2048]{1,0:T(8,128)(2,1)S(1)} %all_gather.27, bf16[2048,4096]{1,0:T(8,128)(2,1)} %get-tuple-element.233), kind=kOutput, calls=%fused_computation.24.clone.1 | convolution fusion | flops 1073741824 | bytes 18087936 | tf_op jit(solution)/shard_map/while/body/eval_jaxpr/dot_general | solution.py:19
  203.1 26.1 %reduce-scatter.2.cloned.1.call-done = f32[64,1024]{1,0:T(8,128)} async-done(((f32[64,4096]{1,0:T(8,128)}), f32[64,1024]{1,0:T(8,128)}) %reduce-scatter.2.cloned.1.call-update) | async-done | bytes 262160 | tf_op jit(solution)/shard_map/while/body/eval_jaxpr/reduce_scatter | solution.py:40
  230.4 5.6 %all_gather.27 = bf16[64,2048]{1,0:T(8,128)(2,1)S(1)} all-gather(bf16[64,1024]{1,0:T(8,128)(2,1)S(1)} %get-tuple-element.221), channel_id=1, replica_groups=mesh['rep'=4,'row'=2,'col'=4] {'row'}, dimensions={1}, use_global_device_ids=true | all-gather | bytes 393216 | tf_op jit(solution)/shard_map/while/body/eval_jaxpr/all_gather | solution.py:36
  236.0 9.8 %fusion.17 = f32[64,4096]{1,0:T(8,128)} fusion(bf16[64,2048]{1,0:T(8,128)(2,1)S(1)} %all_gather.27, bf16[2048,4096]{1,0:T(8,128)(2,1)} %get-tuple-element.233), kind=kOutput, calls=%fused_computation.24.clone.1 | convolution fusion | flops 1073741824 | bytes 18087936 | tf_op jit(solution)/shard_map/while/body/eval_jaxpr/dot_general | solution.py:19
  245.8 26.1 %reduce-scatter.2.cloned.1.call-done = f32[64,1024]{1,0:T(8,128)} async-done(((f32[64,4096]{1,0:T(8,128)}), f32[64,1024]{1,0:T(8,128)}) %reduce-scatter.2.cloned.1.call-update) | async-done | bytes 262160 | tf_op jit(solution)/shard_map/while/body/eval_jaxpr/reduce_scatter | solution.py:40
  273.1 5.6 %all_gather.27 = bf16[64,2048]{1,0:T(8,128)(2,1)S(1)} all-gather(bf16[64,1024]{1,0:T(8,128)(2,1)S(1)} %get-tuple-element.221), channel_id=1, replica_groups=mesh['rep'=4,'row'=2,'col'=4] {'row'}, dimensions={1}, use_global_device_ids=true | all-gather | bytes 393216 | tf_op jit(solution)/shard_map/while/body/eval_jaxpr/all_gather | solution.py:36
  278.8 9.8 %fusion.17 = f32[64,4096]{1,0:T(8,128)} fusion(bf16[64,2048]{1,0:T(8,128)(2,1)S(1)} %all_gather.27, bf16[2048,4096]{1,0:T(8,128)(2,1)} %get-tuple-element.233), kind=kOutput, calls=%fused_computation.24.clone.1 | convolution fusion | flops 1073741824 | bytes 18087936 | tf_op jit(solution)/shard_map/while/body/eval_jaxpr/dot_general | solution.py:19
  288.6 26.1 %reduce-scatter.2.cloned.1.call-done = f32[64,1024]{1,0:T(8,128)} async-done(((f32[64,4096]{1,0:T(8,128)}), f32[64,1024]{1,0:T(8,128)}) %reduce-scatter.2.cloned.1.call-update) | async-done | bytes 262160 | tf_op jit(solution)/shard_map/while/body/eval_jaxpr/reduce_scatter | solution.py:40
  315.9 5.6 %all_gather.27 = bf16[64,2048]{1,0:T(8,128)(2,1)S(1)} all-gather(bf16[64,1024]{1,0:T(8,128)(2,1)S(1)} %get-tuple-element.221), channel_id=1, replica_groups=mesh['rep'=4,'row'=2,'col'=4] {'row'}, dimensions={1}, use_global_device_ids=true | all-gather | bytes 393216 | tf_op jit(solution)/shard_map/while/body/eval_jaxpr/all_gather | solution.py:36
  321.5 9.8 %fusion.17 = f32[64,4096]{1,0:T(8,128)} fusion(bf16[64,2048]{1,0:T(8,128)(2,1)S(1)} %all_gather.27, bf16[2048,4096]{1,0:T(8,128)(2,1)} %get-tuple-element.233), kind=kOutput, calls=%fused_computation.24.clone.1 | convolution fusion | flops 1073741824 | bytes 18087936 | tf_op jit(solution)/shard_map/while/body/eval_jaxpr/dot_general | solution.py:19
  331.3 26.1 %reduce-scatter.2.cloned.1.call-done = f32[64,1024]{1,0:T(8,128)} async-done(((f32[64,4096]{1,0:T(8,128)}), f32[64,1024]{1,0:T(8,128)}) %reduce-scatter.2.cloned.1.call-update) | async-done | bytes 262160 | tf_op jit(solution)/shard_map/while/body/eval_jaxpr/reduce_scatter | solution.py:40
  364.3 9.8 %fusion.17 = f32[64,4096]{1,0:T(8,128)} fusion(bf16[64,2048]{1,0:T(8,128)(2,1)S(1)} %all_gather.27, bf16[2048,4096]{1,0:T(8,128)(2,1)} %get-tuple-element.233), kind=kOutput, calls=%fused_computation.24.clone.1 | convolution fusion | flops 1073741824 | bytes 18087936 | tf_op jit(solution)/shard_map/while/body/eval_jaxpr/dot_general | solution.py:19
  374.1 26.1 %reduce-scatter.2.cloned.1.call-done = f32[64,1024]{1,0:T(8,128)} async-done(((f32[64,4096]{1,0:T(8,128)}), f32[64,1024]{1,0:T(8,128)}) %reduce-scatter.2.cloned.1.call-update) | async-done | bytes 262160 | tf_op jit(solution)/shard_map/while/body/eval_jaxpr/reduce_scatter | solution.py:40
  401.4 5.6 %all_gather.27 = bf16[64,2048]{1,0:T(8,128)(2,1)S(1)} all-gather(bf16[64,1024]{1,0:T(8,128)(2,1)S(1)} %get-tuple-element.221), channel_id=1, replica_groups=mesh['rep'=4,'row'=2,'col'=4] {'row'}, dimensions={1}, use_global_device_ids=true | all-gather | bytes 393216 | tf_op jit(solution)/shard_map/while/body/eval_jaxpr/all_gather | solution.py:36
  407.0 9.8 %fusion.17 = f32[64,4096]{1,0:T(8,128)} fusion(bf16[64,2048]{1,0:T(8,128)(2,1)S(1)} %all_gather.27, bf16[2048,4096]{1,0:T(8,128)(2,1)} %get-tuple-element.233), kind=kOutput, calls=%fused_computation.24.clone.1 | convolution fusion | flops 1073741824 | bytes 18087936 | tf_op jit(solution)/shard_map/while/body/eval_jaxpr/dot_general | solution.py:19
  416.8 26.1 %reduce-scatter.2.cloned.1.call-done = f32[64,1024]{1,0:T(8,128)} async-done(((f32[64,4096]{1,0:T(8,128)}), f32[64,1024]{1,0:T(8,128)}) %reduce-scatter.2.cloned.1.call-update) | async-done | bytes 262160 | tf_op jit(solution)/shard_map/while/body/eval_jaxpr/reduce_scatter | solution.py:40
  449.8 9.8 %fusion.6 = f32[64,4096]{1,0:T(8,128)} fusion(bf16[64,2048]{1,0:T(8,128)(2,1)S(1)} %all_gather.23, bf16[2048,4096]{1,0:T(8,128)(2,1)} %get-tuple-element.241), kind=kOutput, calls=%fused_computation.25 | convolution fusion | flops 1073741824 | bytes 18087936 | tf_op jit(solution)/shard_map/dot_general | solution.py:19
  459.7 20.4 %all_gather.22 = bf16[64,4096]{1,0:T(8,128)(2,1)} all-gather(bf16[64,1024]{1,0:T(8,128)(2,1)S(1)} %get-tuple-element.157), channel_id=1, replica_groups=mesh['rep'=4,'row'=2,'col'=4] {'col'}, dimensions={1}, use_global_device_ids=true | all-gather | bytes 655360 | tf_op jit(solution)/shard_map/all_gather | solution.py:48
  483.0 32.0 %all-reduce.3.cloned.1.call-done = f32[64,4096]{1,0:T(8,128)} async-done(((f32[64,4096]{1,0:T(8,128)}), f32[64,4096]{1,0:T(8,128)}) %all-reduce.3.cloned.1.call-update) | async-done | bytes 1048592 | tf_op jit(solution)/shard_map/psum | solution.py:52
  (78 shorter events, 54.0 us)
Async XLA Ops:
  8.0 1.0 copy-start
  12.4 45.9 %reduce-scatter.2.cloned.1.call-start = ((), (), s32[]{:S(2)}) async-start(), calls=%async_computation.3 | async-start | bytes 1310720 | tf_op jit(solution)/shard_map/while/body/eval_jaxpr/reduce_scatter | solution.py:40
  59.4 41.6 %reduce-scatter.2.cloned.1.call-start = ((), (), s32[]{:S(2)}) async-start(), calls=%async_computation.3 | async-start | bytes 1310720 | tf_op jit(solution)/shard_map/while/body/eval_jaxpr/reduce_scatter | solution.py:40
  102.1 41.6 %reduce-scatter.2.cloned.1.call-start = ((), (), s32[]{:S(2)}) async-start(), calls=%async_computation.3 | async-start | bytes 1310720 | tf_op jit(solution)/shard_map/while/body/eval_jaxpr/reduce_scatter | solution.py:40
  144.9 41.7 %reduce-scatter.2.cloned.1.call-start = ((), (), s32[]{:S(2)}) async-start(), calls=%async_computation.3 | async-start | bytes 1310720 | tf_op jit(solution)/shard_map/while/body/eval_jaxpr/reduce_scatter | solution.py:40
  187.6 41.6 %reduce-scatter.2.cloned.1.call-start = ((), (), s32[]{:S(2)}) async-start(), calls=%async_computation.3 | async-start | bytes 1310720 | tf_op jit(solution)/shard_map/while/body/eval_jaxpr/reduce_scatter | solution.py:40
  230.3 41.6 %reduce-scatter.2.cloned.1.call-start = ((), (), s32[]{:S(2)}) async-start(), calls=%async_computation.3 | async-start | bytes 1310720 | tf_op jit(solution)/shard_map/while/body/eval_jaxpr/reduce_scatter | solution.py:40
  273.1 41.6 %reduce-scatter.2.cloned.1.call-start = ((), (), s32[]{:S(2)}) async-start(), calls=%async_computation.3 | async-start | bytes 1310720 | tf_op jit(solution)/shard_map/while/body/eval_jaxpr/reduce_scatter | solution.py:40
  315.8 41.6 %reduce-scatter.2.cloned.1.call-start = ((), (), s32[]{:S(2)}) async-start(), calls=%async_computation.3 | async-start | bytes 1310720 | tf_op jit(solution)/shard_map/while/body/eval_jaxpr/reduce_scatter | solution.py:40
  358.6 41.6 %reduce-scatter.2.cloned.1.call-start = ((), (), s32[]{:S(2)}) async-start(), calls=%async_computation.3 | async-start | bytes 1310720 | tf_op jit(solution)/shard_map/while/body/eval_jaxpr/reduce_scatter | solution.py:40
  401.3 41.6 %reduce-scatter.2.cloned.1.call-start = ((), (), s32[]{:S(2)}) async-start(), calls=%async_computation.3 | async-start | bytes 1310720 | tf_op jit(solution)/shard_map/while/body/eval_jaxpr/reduce_scatter | solution.py:40
  444.1 36.0 %copy-start.2 = (s32[256]{0:T(256)S(1)}, s32[256]{0:T(256)}, u32[]{:S(2)}) copy-start(s32[256]{0:T(256)} %param.13) | copy-start | bytes 3076
  444.1 36.0 %copy-start.4 = (u32[32]{0:T(128)S(1)}, u32[32]{0:T(128)}, u32[]{:S(2)}) copy-start(u32[32]{0:T(128)} %constant.92) | copy-start | bytes 388
  444.1 37.2 %copy-start.3 = (s32[256]{0:T(256)S(1)}, s32[256]{0:T(256)}, u32[]{:S(2)}) copy-start(s32[256]{0:T(256)} %param.14) | copy-start | bytes 3076
  444.1 37.3 %copy-start.1 = (f32[256]{0:T(256)S(1)}, f32[256]{0:T(256)}, u32[]{:S(2)}) copy-start(f32[256]{0:T(256)} %param.15) | copy-start | bytes 3076
  444.1 70.9 %all-reduce.3.cloned.1.call-start = ((), (), s32[]{:S(2)}) async-start(), calls=%async_computation.1 | async-start | bytes 2097152 | tf_op jit(solution)/shard_map/psum | solution.py:52
  459.6 69.0 %all-gather.2.cloned.1.call-start = ((), (), s32[]{:S(2)}) async-start(), calls=%async_computation.2 | async-start | bytes 2621440 | tf_op jit(solution)/shard_map/all_gather | solution.py:49
Sparse Core Ops, SparseCore 0:
  29.5 28.7 reduce-scatter.1
  75.0 25.9 reduce-scatter.1
  117.7 25.9 reduce-scatter.1
  160.5 26.0 reduce-scatter.1
  203.2 25.9 reduce-scatter.1
  246.0 25.9 reduce-scatter.1
  288.7 25.9 reduce-scatter.1
  331.4 25.9 reduce-scatter.1
  374.2 25.9 reduce-scatter.1
  416.9 25.9 reduce-scatter.1
  480.2 21.6 all-gather.1
Sparse Core Ops, SparseCore 1:
  459.7 55.3 all-reduce.2
where the time goes:
time: 542 us; the launch traced here: 541 us
  waiting for transfers between devices  296 us (55%)
  matrix products  107 us (20%)
  blocking collectives  94.4 us (17%)
  other arithmetic  16 us (3%)
  between operations  15.9 us (3%)
  local copies, waits for them, and re-layouts  9.87 us (2%)
    reduce_scatter x10, waiting for transfers between devices, one_sweep(): fields = lax.psum_scatter(terms, 'col', scatter_dimension=1, tiled=True)  264 us
    dot_general x11, matrix products, partial_fields(): return jnp.dot(strided, coupling_block, preferred_element_type=jnp.float32)  107 us
    all_gather x11, blocking collectives, strided_of(): return lax.all_gather(spin_state, 'row', axis=1, tiled=True)  63.5 us
    psum x1, waiting for transfers between devices, per_device(): final_local = lax.psum(final_partial, 'col')  32 us
    all_gather x1, blocking collectives, per_device(): final_rows = lax.all_gather(final_pieces, 'col', axis=1, tiled=True)  20.4 us
    convert_element_type x10, other arithmetic, metropolis(): return jnp.where(flipped, -values, values).astype(jnp.bfloat16)  10.9 us
  transfers between devices with their start and end apart: 12, of which 11 were waited for; matrix products, arithmetic and copies ran while one was open for 1% of the time, Pallas kernels for 0%

commit v1 on v0

--- a/solution.py
+++ b/solution.py
@@ -6,6 +6,13 @@
 
 N = 8192
 SWEEPS = 10
+
+
+def exchange_gather(value, mesh_axis, dim):
+    size = lax.axis_size(mesh_axis)
+    blocks = jnp.stack([value for _ in range(size)])
+    blocks = lax.all_to_all(blocks, mesh_axis, split_axis=0, concat_axis=0)
+    return jnp.concatenate(blocks, axis=dim)
 
 
 def metropolis(spin_state, fields, parity, color_part, noise_part, beta_col):
@@ -33,7 +40,7 @@
     noise_part = lax.dynamic_slice_in_dim(flip_noise, col_index * piece_size, piece_size, 2)
 
     def strided_of(spin_state):
-        return lax.all_gather(spin_state, "row", axis=1, tiled=True)
+        return exchange_gather(spin_state, "row", 1)
 
     def one_sweep(step_index, spin_state):
         terms = partial_fields(strided_of(spin_state), coupling_block)

time: 542 us -> 554 us (1.022)
  blocking collectives: 94.4 us -> 117 us
  waiting for transfers between devices: 296 us -> 285 us
    all_to_all x0 -> x11, blocking collectives: none -> 86.3 us  [exchange_gather(): blocks = lax.all_to_all(blocks, mesh_axis, split_axis=0, concat_axis=0)]
    all_gather x11 -> x0, blocking collectives: 63.5 us -> none  [strided_of(): return lax.all_gather(spin_state, 'row', axis=1, tiled=True)]
    reduce_scatter x10, waiting for transfers between devices: 264 us -> 254 us  [one_sweep(): fields = lax.psum_scatter(terms, 'col', scatter_dimension=1, tiled=True)]
where the time goes in v1:
time: 554 us; the launch traced here: 553 us
  waiting for transfers between devices  285 us (51%)
  blocking collectives  117 us (21%)
  matrix products  107 us (19%)
  other arithmetic  16.2 us (3%)
  between operations  15.9 us (3%)
  local copies, waits for them, and re-layouts  10.1 us (2%)
    reduce_scatter x10, waiting for transfers between devices, one_sweep(): fields = lax.psum_scatter(terms, 'col', scatter_dimension=1, tiled=True)  254 us
    dot_general x11, matrix products, partial_fields(): return jnp.dot(strided, coupling_block, preferred_element_type=jnp.float32)  107 us
    all_to_all x11, blocking collectives, exchange_gather(): blocks = lax.all_to_all(blocks, mesh_axis, split_axis=0, concat_axis=0)  86.3 us
    psum x1, waiting for transfers between devices, per_device(): final_local = lax.psum(final_partial, 'col')  30.9 us
    all_gather x1, blocking collectives, per_device(): final_rows = lax.all_gather(final_pieces, 'col', axis=1, tiled=True)  20.3 us
  transfers between devices with their start and end apart: 12, of which 11 were waited for; matrix products, arithmetic and copies ran while one was open for 1% of the time, Pallas kernels for 0%

profile of v1, /device:TPU:0, one launch (start us, length us, event | category | flops | bytes accessed | tf_op | source)
XLA Modules:
  0.0 552.6 jit_solution(15252093343678648281)
XLA Ops:
  12.4 442.3 %while.15 = (s32[]{:T(128)}, bf16[64,1024]{1,0:T(8,128)(2,1)S(1)}, s32[1024]{0:T(1024)S(1)}, f32[64,1]{0,1:T(1,128)S(1)}, bf16[2048,4096]{1,0:T(8,128)(2,1)}, /*...) while((s32[]{:T(128)}, bf16[64,1024]{1,0:T(8,128)(2,1)S(1)}, s32[1024]{0:T(1024)S(1)}, ...), condition=%wide.region_2.3_spmd, body=%wide.region_0.2_spmd.sunk | while | flops 1074463744 | bytes 24254924 | solution.py:53
  12.5 9.2 %all_to_all.19 = bf16[2,64,1024]{2,1,0:T(8,128)(2,1)S(1)} all-to-all(bf16[2,64,1024]{2,1,0:T(8,128)(2,1)S(1)} %pad_maximum_fusion.3), channel_id=1, replica_groups=mesh['rep'=4,'row'=2,'col'=4] {'row'}, dimensions={0} | all-to-all | bytes 524288 | tf_op jit(solution)/shard_map/while/body/eval_jaxpr/all_to_all | solution.py:14
  21.7 9.8 %fusion.17 = f32[64,4096]{1,0:T(8,128)} fusion(bf16[64,2048]{1,0:T(8,128)(2,1)S(1)} %bitcast.36, bf16[2048,4096]{1,0:T(8,128)(2,1)} %get-tuple-element.233), kind=kOutput, calls=%fused_computation.26.clone.1 | convolution fusion | flops 1073741824 | bytes 18087936 | tf_op jit(solution)/shard_map/while/body/eval_jaxpr/dot_general | solution.py:26
  31.5 27.8 %reduce-scatter.2.cloned.1.call-done = f32[64,1024]{1,0:T(8,128)} async-done(((f32[64,4096]{1,0:T(8,128)}), f32[64,1024]{1,0:T(8,128)}) %reduce-scatter.2.cloned.1.call-update) | async-done | bytes 262160 | tf_op jit(solution)/shard_map/while/body/eval_jaxpr/reduce_scatter | solution.py:47
  60.5 7.7 %all_to_all.19 = bf16[2,64,1024]{2,1,0:T(8,128)(2,1)S(1)} all-to-all(bf16[2,64,1024]{2,1,0:T(8,128)(2,1)S(1)} %pad_maximum_fusion.3), channel_id=1, replica_groups=mesh['rep'=4,'row'=2,'col'=4] {'row'}, dimensions={0} | all-to-all | bytes 524288 | tf_op jit(solution)/shard_map/while/body/eval_jaxpr/all_to_all | solution.py:14
  68.2 9.8 %fusion.17 = f32[64,4096]{1,0:T(8,128)} fusion(bf16[64,2048]{1,0:T(8,128)(2,1)S(1)} %bitcast.36, bf16[2048,4096]{1,0:T(8,128)(2,1)} %get-tuple-element.233), kind=kOutput, calls=%fused_computation.26.clone.1 | convolution fusion | flops 1073741824 | bytes 18087936 | tf_op jit(solution)/shard_map/while/body/eval_jaxpr/dot_general | solution.py:26
  78.1 25.1 %reduce-scatter.2.cloned.1.call-done = f32[64,1024]{1,0:T(8,128)} async-done(((f32[64,4096]{1,0:T(8,128)}), f32[64,1024]{1,0:T(8,128)}) %reduce-scatter.2.cloned.1.call-update) | async-done | bytes 262160 | tf_op jit(solution)/shard_map/while/body/eval_jaxpr/reduce_scatter | solution.py:47
  104.3 7.7 %all_to_all.19 = bf16[2,64,1024]{2,1,0:T(8,128)(2,1)S(1)} all-to-all(bf16[2,64,1024]{2,1,0:T(8,128)(2,1)S(1)} %pad_maximum_fusion.3), channel_id=1, replica_groups=mesh['rep'=4,'row'=2,'col'=4] {'row'}, dimensions={0} | all-to-all | bytes 524288 | tf_op jit(solution)/shard_map/while/body/eval_jaxpr/all_to_all | solution.py:14
  112.1 9.8 %fusion.17 = f32[64,4096]{1,0:T(8,128)} fusion(bf16[64,2048]{1,0:T(8,128)(2,1)S(1)} %bitcast.36, bf16[2048,4096]{1,0:T(8,128)(2,1)} %get-tuple-element.233), kind=kOutput, calls=%fused_computation.26.clone.1 | convolution fusion | flops 1073741824 | bytes 18087936 | tf_op jit(solution)/shard_map/while/body/eval_jaxpr/dot_general | solution.py:26
  121.9 25.1 %reduce-scatter.2.cloned.1.call-done = f32[64,1024]{1,0:T(8,128)} async-done(((f32[64,4096]{1,0:T(8,128)}), f32[64,1024]{1,0:T(8,128)}) %reduce-scatter.2.cloned.1.call-update) | async-done | bytes 262160 | tf_op jit(solution)/shard_map/while/body/eval_jaxpr/reduce_scatter | solution.py:47
  148.2 7.7 %all_to_all.19 = bf16[2,64,1024]{2,1,0:T(8,128)(2,1)S(1)} all-to-all(bf16[2,64,1024]{2,1,0:T(8,128)(2,1)S(1)} %pad_maximum_fusion.3), channel_id=1, replica_groups=mesh['rep'=4,'row'=2,'col'=4] {'row'}, dimensions={0} | all-to-all | bytes 524288 | tf_op jit(solution)/shard_map/while/body/eval_jaxpr/all_to_all | solution.py:14
  155.9 9.8 %fusion.17 = f32[64,4096]{1,0:T(8,128)} fusion(bf16[64,2048]{1,0:T(8,128)(2,1)S(1)} %bitcast.36, bf16[2048,4096]{1,0:T(8,128)(2,1)} %get-tuple-element.233), kind=kOutput, calls=%fused_computation.26.clone.1 | convolution fusion | flops 1073741824 | bytes 18087936 | tf_op jit(solution)/shard_map/while/body/eval_jaxpr/dot_general | solution.py:26
  165.7 25.1 %reduce-scatter.2.cloned.1.call-done = f32[64,1024]{1,0:T(8,128)} async-done(((f32[64,4096]{1,0:T(8,128)}), f32[64,1024]{1,0:T(8,128)}) %reduce-scatter.2.cloned.1.call-update) | async-done | bytes 262160 | tf_op jit(solution)/shard_map/while/body/eval_jaxpr/reduce_scatter | solution.py:47
  199.7 9.8 %fusion.17 = f32[64,4096]{1,0:T(8,128)} fusion(bf16[64,2048]{1,0:T(8,128)(2,1)S(1)} %bitcast.36, bf16[2048,4096]{1,0:T(8,128)(2,1)} %get-tuple-element.233), kind=kOutput, calls=%fused_computation.26.clone.1 | convolution fusion | flops 1073741824 | bytes 18087936 | tf_op jit(solution)/shard_map/while/body/eval_jaxpr/dot_general | solution.py:26
  209.5 25.1 %reduce-scatter.2.cloned.1.call-done = f32[64,1024]{1,0:T(8,128)} async-done(((f32[64,4096]{1,0:T(8,128)}), f32[64,1024]{1,0:T(8,128)}) %reduce-scatter.2.cloned.1.call-update) | async-done | bytes 262160 | tf_op jit(solution)/shard_map/while/body/eval_jaxpr/reduce_scatter | solution.py:47
  235.8 7.7 %all_to_all.19 = bf16[2,64,1024]{2,1,0:T(8,128)(2,1)S(1)} all-to-all(bf16[2,64,1024]{2,1,0:T(8,128)(2,1)S(1)} %pad_maximum_fusion.3), channel_id=1, replica_groups=mesh['rep'=4,'row'=2,'col'=4] {'row'}, dimensions={0} | all-to-all | bytes 524288 | tf_op jit(solution)/shard_map/while/body/eval_jaxpr/all_to_all | solution.py:14
  243.5 9.8 %fusion.17 = f32[64,4096]{1,0:T(8,128)} fusion(bf16[64,2048]{1,0:T(8,128)(2,1)S(1)} %bitcast.36, bf16[2048,4096]{1,0:T(8,128)(2,1)} %get-tuple-element.233), kind=kOutput, calls=%fused_computation.26.clone.1 | convolution fusion | flops 1073741824 | bytes 18087936 | tf_op jit(solution)/shard_map/while/body/eval_jaxpr/dot_general | solution.py:26
  253.3 25.1 %reduce-scatter.2.cloned.1.call-done = f32[64,1024]{1,0:T(8,128)} async-done(((f32[64,4096]{1,0:T(8,128)}), f32[64,1024]{1,0:T(8,128)}) %reduce-scatter.2.cloned.1.call-update) | async-done | bytes 262160 | tf_op jit(solution)/shard_map/while/body/eval_jaxpr/reduce_scatter | solution.py:47
  279.6 7.7 %all_to_all.19 = bf16[2,64,1024]{2,1,0:T(8,128)(2,1)S(1)} all-to-all(bf16[2,64,1024]{2,1,0:T(8,128)(2,1)S(1)} %pad_maximum_fusion.3), channel_id=1, replica_groups=mesh['rep'=4,'row'=2,'col'=4] {'row'}, dimensions={0} | all-to-all | bytes 524288 | tf_op jit(solution)/shard_map/while/body/eval_jaxpr/all_to_all | solution.py:14
  287.3 9.8 %fusion.17 = f32[64,4096]{1,0:T(8,128)} fusion(bf16[64,2048]{1,0:T(8,128)(2,1)S(1)} %bitcast.36, bf16[2048,4096]{1,0:T(8,128)(2,1)} %get-tuple-element.233), kind=kOutput, calls=%fused_computation.26.clone.1 | convolution fusion | flops 1073741824 | bytes 18087936 | tf_op jit(solution)/shard_map/while/body/eval_jaxpr/dot_general | solution.py:26
  297.1 25.1 %reduce-scatter.2.cloned.1.call-done = f32[64,1024]{1,0:T(8,128)} async-done(((f32[64,4096]{1,0:T(8,128)}), f32[64,1024]{1,0:T(8,128)}) %reduce-scatter.2.cloned.1.call-update) | async-done | bytes 262160 | tf_op jit(solution)/shard_map/while/body/eval_jaxpr/reduce_scatter | solution.py:47
  323.4 7.7 %all_to_all.19 = bf16[2,64,1024]{2,1,0:T(8,128)(2,1)S(1)} all-to-all(bf16[2,64,1024]{2,1,0:T(8,128)(2,1)S(1)} %pad_maximum_fusion.3), channel_id=1, replica_groups=mesh['rep'=4,'row'=2,'col'=4] {'row'}, dimensions={0} | all-to-all | bytes 524288 | tf_op jit(solution)/shard_map/while/body/eval_jaxpr/all_to_all | solution.py:14
  331.1 9.8 %fusion.17 = f32[64,4096]{1,0:T(8,128)} fusion(bf16[64,2048]{1,0:T(8,128)(2,1)S(1)} %bitcast.36, bf16[2048,4096]{1,0:T(8,128)(2,1)} %get-tuple-element.233), kind=kOutput, calls=%fused_computation.26.clone.1 | convolution fusion | flops 1073741824 | bytes 18087936 | tf_op jit(solution)/shard_map/while/body/eval_jaxpr/dot_general | solution.py:26
  340.9 25.1 %reduce-scatter.2.cloned.1.call-done = f32[64,1024]{1,0:T(8,128)} async-done(((f32[64,4096]{1,0:T(8,128)}), f32[64,1024]{1,0:T(8,128)}) %reduce-scatter.2.cloned.1.call-update) | async-done | bytes 262160 | tf_op jit(solution)/shard_map/while/body/eval_jaxpr/reduce_scatter | solution.py:47
  367.2 7.7 %all_to_all.19 = bf16[2,64,1024]{2,1,0:T(8,128)(2,1)S(1)} all-to-all(bf16[2,64,1024]{2,1,0:T(8,128)(2,1)S(1)} %pad_maximum_fusion.3), channel_id=1, replica_groups=mesh['rep'=4,'row'=2,'col'=4] {'row'}, dimensions={0} | all-to-all | bytes 524288 | tf_op jit(solution)/shard_map/while/body/eval_jaxpr/all_to_all | solution.py:14
  374.9 9.8 %fusion.17 = f32[64,4096]{1,0:T(8,128)} fusion(bf16[64,2048]{1,0:T(8,128)(2,1)S(1)} %bitcast.36, bf16[2048,4096]{1,0:T(8,128)(2,1)} %get-tuple-element.233), kind=kOutput, calls=%fused_computation.26.clone.1 | convolution fusion | flops 1073741824 | bytes 18087936 | tf_op jit(solution)/shard_map/while/body/eval_jaxpr/dot_general | solution.py:26
  384.7 25.1 %reduce-scatter.2.cloned.1.call-done = f32[64,1024]{1,0:T(8,128)} async-done(((f32[64,4096]{1,0:T(8,128)}), f32[64,1024]{1,0:T(8,128)}) %reduce-scatter.2.cloned.1.call-update) | async-done | bytes 262160 | tf_op jit(solution)/shard_map/while/body/eval_jaxpr/reduce_scatter | solution.py:47
  418.7 9.8 %fusion.17 = f32[64,4096]{1,0:T(8,128)} fusion(bf16[64,2048]{1,0:T(8,128)(2,1)S(1)} %bitcast.36, bf16[2048,4096]{1,0:T(8,128)(2,1)} %get-tuple-element.233), kind=kOutput, calls=%fused_computation.26.clone.1 | convolution fusion | flops 1073741824 | bytes 18087936 | tf_op jit(solution)/shard_map/while/body/eval_jaxpr/dot_general | solution.py:26
  428.6 25.1 %reduce-scatter.2.cloned.1.call-done = f32[64,1024]{1,0:T(8,128)} async-done(((f32[64,4096]{1,0:T(8,128)}), f32[64,1024]{1,0:T(8,128)}) %reduce-scatter.2.cloned.1.call-update) | async-done | bytes 262160 | tf_op jit(solution)/shard_map/while/body/eval_jaxpr/reduce_scatter | solution.py:47
  462.6 9.8 %fusion.6 = f32[64,4096]{1,0:T(8,128)} fusion(bf16[64,2048]{1,0:T(8,128)(2,1)S(1)} %bitcast.40, bf16[2048,4096]{1,0:T(8,128)(2,1)} %get-tuple-element.241), kind=kOutput, calls=%fused_computation.27 | convolution fusion | flops 1073741824 | bytes 18087936 | tf_op jit(solution)/shard_map/dot_general | solution.py:26
  472.5 20.3 %all_gather.9 = bf16[64,4096]{1,0:T(8,128)(2,1)} all-gather(bf16[64,1024]{1,0:T(8,128)(2,1)S(1)} %get-tuple-element.157), channel_id=1, replica_groups=mesh['rep'=4,'row'=2,'col'=4] {'col'}, dimensions={1}, use_global_device_ids=true | all-gather | bytes 655360 | tf_op jit(solution)/shard_map/all_gather | solution.py:55
  495.7 30.9 %all-reduce.3.cloned.1.call-done = f32[64,4096]{1,0:T(8,128)} async-done(((f32[64,4096]{1,0:T(8,128)}), f32[64,4096]{1,0:T(8,128)}) %all-reduce.3.cloned.1.call-update) | async-done | bytes 1048592 | tf_op jit(solution)/shard_map/psum | solution.py:59
  (100 shorter events, 60.6 us)
Async XLA Ops:
  8.0 1.0 copy-start
  12.4 46.9 %reduce-scatter.2.cloned.1.call-start = ((), (), s32[]{:S(2)}) async-start(), calls=%async_computation.5 | async-start | bytes 1310720 | tf_op jit(solution)/shard_map/while/body/eval_jaxpr/reduce_scatter | solution.py:47
  60.4 42.7 %reduce-scatter.2.cloned.1.call-start = ((), (), s32[]{:S(2)}) async-start(), calls=%async_computation.5 | async-start | bytes 1310720 | tf_op jit(solution)/shard_map/while/body/eval_jaxpr/reduce_scatter | solution.py:47
  104.2 42.7 %reduce-scatter.2.cloned.1.call-start = ((), (), s32[]{:S(2)}) async-start(), calls=%async_computation.5 | async-start | bytes 1310720 | tf_op jit(solution)/shard_map/while/body/eval_jaxpr/reduce_scatter | solution.py:47
  148.1 42.7 %reduce-scatter.2.cloned.1.call-start = ((), (), s32[]{:S(2)}) async-start(), calls=%async_computation.5 | async-start | bytes 1310720 | tf_op jit(solution)/shard_map/while/body/eval_jaxpr/reduce_scatter | solution.py:47
  191.9 42.7 %reduce-scatter.2.cloned.1.call-start = ((), (), s32[]{:S(2)}) async-start(), calls=%async_computation.5 | async-start | bytes 1310720 | tf_op jit(solution)/shard_map/while/body/eval_jaxpr/reduce_scatter | solution.py:47
  235.7 42.7 %reduce-scatter.2.cloned.1.call-start = ((), (), s32[]{:S(2)}) async-start(), calls=%async_computation.5 | async-start | bytes 1310720 | tf_op jit(solution)/shard_map/while/body/eval_jaxpr/reduce_scatter | solution.py:47
  279.5 42.7 %reduce-scatter.2.cloned.1.call-start = ((), (), s32[]{:S(2)}) async-start(), calls=%async_computation.5 | async-start | bytes 1310720 | tf_op jit(solution)/shard_map/while/body/eval_jaxpr/reduce_scatter | solution.py:47
  323.3 42.7 %reduce-scatter.2.cloned.1.call-start = ((), (), s32[]{:S(2)}) async-start(), calls=%async_computation.5 | async-start | bytes 1310720 | tf_op jit(solution)/shard_map/while/body/eval_jaxpr/reduce_scatter | solution.py:47
  367.1 42.7 %reduce-scatter.2.cloned.1.call-start = ((), (), s32[]{:S(2)}) async-start(), calls=%async_computation.5 | async-start | bytes 1310720 | tf_op jit(solution)/shard_map/while/body/eval_jaxpr/reduce_scatter | solution.py:47
  410.9 42.7 %reduce-scatter.2.cloned.1.call-start = ((), (), s32[]{:S(2)}) async-start(), calls=%async_computation.5 | async-start | bytes 1310720 | tf_op jit(solution)/shard_map/while/body/eval_jaxpr/reduce_scatter | solution.py:47
  454.8 38.0 %copy-start.2 = (s32[256]{0:T(256)S(1)}, s32[256]{0:T(256)}, u32[]{:S(2)}) copy-start(s32[256]{0:T(256)} %param.13) | copy-start | bytes 3076
  454.8 38.0 %copy-start.4 = (u32[32]{0:T(128)S(1)}, u32[32]{0:T(128)}, u32[]{:S(2)}) copy-start(u32[32]{0:T(128)} %constant.92) | copy-start | bytes 388
  454.8 39.2 %copy-start.3 = (s32[256]{0:T(256)S(1)}, s32[256]{0:T(256)}, u32[]{:S(2)}) copy-start(s32[256]{0:T(256)} %param.14) | copy-start | bytes 3076
  454.8 39.3 %copy-start.1 = (f32[256]{0:T(256)S(1)}, f32[256]{0:T(256)}, u32[]{:S(2)}) copy-start(f32[256]{0:T(256)} %param.15) | copy-start | bytes 3076
  454.8 71.8 %all-reduce.3.cloned.1.call-start = ((), (), s32[]{:S(2)}) async-start(), calls=%async_computation.3 | async-start | bytes 2097152 | tf_op jit(solution)/shard_map/psum | solution.py:59
  472.4 67.9 %all-gather.2.cloned.1.call-start = ((), (), s32[]{:S(2)}) async-start(), calls=%async_computation.4 | async-start | bytes 2621440 | tf_op jit(solution)/shard_map/all_gather | solution.py:56
Sparse Core Ops, SparseCore 0:
  31.6 27.6 reduce-scatter.1
  78.2 24.9 reduce-scatter.1
  122.0 24.9 reduce-scatter.1
  165.8 24.9 reduce-scatter.1
  209.6 24.9 reduce-scatter.1
  253.4 24.9 reduce-scatter.1
  297.2 24.9 reduce-scatter.1
  341.0 24.9 reduce-scatter.1
  384.8 24.9 reduce-scatter.1
  428.7 24.9 reduce-scatter.1
  492.9 21.1 all-gather.1
Sparse Core Ops, SparseCore 1:
  472.5 54.1 all-reduce.2
